TPU v7x, 256 devices: a whole 4x4x8 slice. The times are simulated.
256 devices in a mesh: mp: 32 (over x, z), dp: 8 (over y, core).
Axes of the slice: x: 4, y: 4, z: 8, core: 2. Of those that a mesh axis runs over, the one named last changes fastest.
Arguments:
- tables: bfloat16 [20, 65536, 128], P(None, 'mp'), may hold values from -3 to 3
- block_rows: int32 [16384, 128], P(('mp', 'dp')), may hold values from 0 to 2047
- block_slots: int32 [16384, 128], P(('mp', 'dp')), may hold values from 0 to 127
- block_table: int32 [16384], P(('mp', 'dp')), may hold values from 0 to 19
- block_peer: int32 [16384, 1], P(('mp', 'dp')), may hold values from 0 to 31; in each aligned block of 64 rows (0 to 63, 64 to 127, ...) at most 4 rows name the same one
- block_len: int32 [16384], P(('mp', 'dp')), may hold values from 1 to 128
- block_count: int32 [256], P(('mp', 'dp')), may hold values from 1 to 64, as said below
- cross_in: bfloat16 [4, 2560, 256], P(None, 'dp'), may hold values from -0.23632812 to 0.23632812
- cross_mix: bfloat16 [4, 256, 256], replicated, may hold values from -0.5625 to 0.5625
- cross_out: bfloat16 [4, 256, 2560], P(None, None, 'dp'), may hold values from -0.375 to 0.375
- cross_bias: float32 [4, 2560], replicated, may hold values from -3 to 3
- gate_weight: bfloat16 [4, 2560], replicated, may hold values from -0.47265625 to 0.47265625
Outputs:
- crossed: bfloat16 [32768, 2560], P(('mp', 'dp'))
Inputs may be any that keep to these rules, and one draw needn't show every extreme that they name: `block_peer`: in the 64 blocks of one device no destination is named by more than 4 blocks, a bound that the blocks of some device reach. The live blocks of a device are its first block_count blocks; some device has exactly 64. Entries of a block at positions below its block_len are live. `block_rows`: A row index within the device's own shard of the table. `block_slots`: A sample of the destination device.
All inputs are finite; a program needn't handle non-finite values.
Results may differ from a plain program's by a relative error of at most 0.0059.
Values may be sent and summed in bfloat16 or wider, within the bound.
A program may use at most 128 MiB of HBM per device.

v0:
```python
import jax
import jax.numpy as jnp
from jax import lax
from jax.sharding import PartitionSpec as P

B_DEV = 128


blocks_per_turn = 8


def pick_rows(tables, block_rows, block_table, first):
    row_ids = lax.dynamic_slice_in_dim(block_rows, first, blocks_per_turn, 0)
    table_ids = lax.dynamic_slice_in_dim(block_table, first, blocks_per_turn, 0)
    return tables[table_ids[:, None], row_ids]


def on_device(
    tables,
    block_rows,
    block_slots,
    block_table,
    block_peer,
    block_len,
    block_count,
    cross_in,
    cross_mix,
    cross_out,
    cross_bias,
    gate_weight,
):
    peers = lax.axis_size("mp")
    total_blocks, block_width = block_rows.shape
    table_count, rows_dev, width = tables.shape
    samples = B_DEV
    count = block_count[0]
    turns = (count + blocks_per_turn - 1) // blocks_per_turn
    peer_ids = block_peer[:, 0]
    entries = jnp.arange(block_width, dtype=jnp.int32)
    sample_ids = jnp.arange(samples, dtype=jnp.int32)
    capacity = max(2, 2 * total_blocks // peers)

    def gather_turn(turn, store):
        first = turn * blocks_per_turn
        picked = pick_rows(tables, block_rows, block_table, first)
        return lax.dynamic_update_slice_in_dim(store, picked, first, 0)

    stored = lax.fori_loop(
        0, turns, gather_turn, jnp.zeros((total_blocks, block_width, width), jnp.bfloat16)
    )
    live_block = jnp.arange(total_blocks, dtype=jnp.int32) < count
    peer_table = (
        (peer_ids[:, None] == jnp.arange(peers, dtype=jnp.int32)[None, :]) & live_block[:, None]
    ).astype(jnp.int32)
    before = jnp.cumsum(peer_table, axis=0) - peer_table
    position = jnp.sum(before * peer_table, axis=1)
    target = jnp.where(live_block, peer_ids * capacity + position, peers * capacity)
    live_entry = (entries[None, :] < block_len[:, None]) & live_block[:, None]
    code = jnp.where(live_entry, block_table[:, None] * samples + block_slots, -1)
    send_rows = (
        jnp.zeros((peers * capacity, block_width, width), jnp.bfloat16)
        .at[target]
        .set(stored, mode="drop")
    )
    send_code = (
        jnp.full((peers * capacity, block_width), -1, jnp.int32).at[target].set(code, mode="drop")
    )
    arrived_rows, arrived_code = (
        lax.all_to_all(
            send_rows.reshape(peers, capacity, block_width, width),
            "mp",
            split_axis=0,
            concat_axis=0,
            tiled=True,
        ),
        lax.all_to_all(
            send_code.reshape(peers, capacity, block_width),
            "mp",
            split_axis=0,
            concat_axis=0,
            tiled=True,
        ),
    )
    flat_rows = arrived_rows.reshape(peers * capacity, block_width, width)
    flat_code = arrived_code.reshape(peers * capacity, block_width)
    slot_of = jnp.where(flat_code >= 0, flat_code % samples, -1)
    onehot = (slot_of[:, :, None] == sample_ids[None, None, :]).astype(jnp.bfloat16)
    contrib = jnp.einsum("kis,kiw->ksw", onehot, flat_rows, preferred_element_type=jnp.float32)
    top_code = jnp.max(flat_code, axis=1)
    slot_live = top_code >= 0
    table_of = jnp.maximum(top_code, 0) // samples
    table_grid = table_of.reshape(peers, capacity)
    live_grid = slot_live.reshape(peers, capacity)
    same = (
        (table_grid[:, :, None] == table_grid[:, None, :])
        & live_grid[:, :, None]
        & live_grid[:, None, :]
    )
    grouped = jnp.einsum(
        "pkj,pjx->pkx", same.astype(jnp.float32), contrib.reshape(peers, capacity, samples * width)
    )
    rounded = grouped.astype(jnp.bfloat16).astype(jnp.float32)
    slot_order = jnp.arange(capacity, dtype=jnp.int32)
    earlier = jnp.sum(same & (slot_order[None, None, :] < slot_order[None, :, None]), axis=2)
    leader = (live_grid & (earlier == 0)).reshape(peers * capacity)
    owner = (
        (table_of[:, None] == jnp.arange(table_count, dtype=jnp.int32)[None, :]) & leader[:, None]
    ).astype(jnp.float32)
    summed = jnp.einsum("kt,kx->tx", owner, rounded.reshape(peers * capacity, samples * width))
    embedded = (
        summed.reshape(table_count, samples, width)
        .transpose(1, 0, 2)
        .reshape(samples, table_count * width)
        .astype(jnp.bfloat16)
    )
    gate = jax.nn.sigmoid(jnp.dot(embedded, gate_weight.T, preferred_element_type=jnp.float32))
    projected = jnp.einsum(
        "bn,enr->ebr",
        embedded,
        lax.all_gather(cross_in, "dp", axis=1, tiled=True),
        preferred_element_type=jnp.float32,
    )
    hidden = jnp.tanh(projected).astype(jnp.bfloat16)
    mixed = jnp.tanh(
        jnp.einsum("ebr,erq->ebq", hidden, cross_mix, preferred_element_type=jnp.float32)
    ).astype(jnp.bfloat16)
    gate_columns = gate.T
    grown = jnp.einsum(
        "ebr,ern->ebn",
        mixed,
        lax.all_gather(cross_out, "dp", axis=2, tiled=True),
        preferred_element_type=jnp.float32,
    )
    grown = grown + cross_bias[:, None, :]
    weighted = jnp.sum(gate_columns[:, :, None] * grown, axis=0)
    base = embedded.astype(jnp.float32)
    return (base + base * weighted).astype(jnp.bfloat16)


def solution(mesh):
    in_specs = (
        P(None, "mp", None),
        P(("mp", "dp"), None),
        P(("mp", "dp"), None),
        P(("mp", "dp")),
        P(("mp", "dp"), None),
        P(("mp", "dp")),
        P(("mp", "dp")),
        P(None, "dp", None),
        P(),
        P(None, None, "dp"),
        P(),
        P(),
    )
    out_specs = P(("mp", "dp"), None)
    return jax.shard_map(
        on_device, mesh=mesh, in_specs=in_specs, out_specs=out_specs, check_vma=False
    )
```

profile of v0, /device:TPU:8, one launch (start us, length us, event | category | flops | bytes accessed | tf_op | source)
XLA Modules:
  0.0 309.9 jit_solution(1499856670255202471)
XLA Ops:
  6.5 0.0 copy-start
  6.5 0.0 all-gather.3.cloned.1.call-start
  6.5 0.7 all-gather.3.cloned.1.call-update
  7.9 0.7 fusion.25
  8.7 0.1 reduce_window_sum.11
  8.8 0.8 select_reduce_fusion
  9.6 0.7 broadcast_multiply_fusion
  10.3 0.7 fusion.38
  10.9 1.6 scatter_custom_fusion
  12.6 11.3 %all-to-all-start = ((s32[32,4,128]{2,1,0:T(4,128)}), s32[32,4,128]{2,1,0:T(4,128)S(1)}, u32[]{:S(2)}, u32[]{:S(2)}) async-start(s32[32,4,128]{2,1,0:T(4,128)} %bitcast.7), calls=%async_computation | async-start | bytes 131072 | tf_op jit(solution)/shard_map/all_to_all | solution.py:76
  23.9 0.5 broadcast_in_dim.29
  24.4 43.7 %while.10 = (s32[]{:T(128)}, bf16[64,128,128]{2,1,0:T(8,128)(2,1)S(1)}, s32[]{:T(128)}, s32[64]{0:T(128)}, s32[64,128]{1,0:T(8,128)}, /*index=5*/bf16[20,2048,12...) while((s32[]{:T(128)}, bf16[64,128,128]{2,1,0:T(8,128)(2,1)S(1)}, s32[]{:T(128)}, ...), condition=%wide.region_6.7_spmd, body=%wide.region_5.6_spmd.sunk | while | flops 6190 | bytes 1065215 | solution.py:48
  24.4 0.7 fusion.52
  25.2 0.8 fusion.53
  25.9 12.9 %gather_fusion = bf16[1024,128]{1,0:T(8,128)(2,1)S(1)} fusion(bf16[20,2048,128]{2,1,0:T(8,128)(2,1)} %get-tuple-element.117, s32[1024]{0:T(1024)S(1)} %fusion.53), kind=kCustom, calls=%fused_computation.clone.1 | custom fusion | bytes 532480 | tf_op jit(solution)/shard_map/while/body/gather | solution.py:15
  38.9 0.7 fusion.52
  39.7 0.8 fusion.53
  40.4 12.9 %gather_fusion = bf16[1024,128]{1,0:T(8,128)(2,1)S(1)} fusion(bf16[20,2048,128]{2,1,0:T(8,128)(2,1)} %get-tuple-element.117, s32[1024]{0:T(1024)S(1)} %fusion.53), kind=kCustom, calls=%fused_computation.clone.1 | custom fusion | bytes 532480 | tf_op jit(solution)/shard_map/while/body/gather | solution.py:15
  53.4 0.7 fusion.52
  54.1 0.8 fusion.53
  54.8 13.2 %gather_fusion = bf16[1024,128]{1,0:T(8,128)(2,1)S(1)} fusion(bf16[20,2048,128]{2,1,0:T(8,128)(2,1)} %get-tuple-element.117, s32[1024]{0:T(1024)S(1)} %fusion.53), kind=kCustom, calls=%fused_computation.clone.1 | custom fusion | bytes 532480 | tf_op jit(solution)/shard_map/while/body/gather | solution.py:15
  68.1 3.0 broadcast_in_dim.28
  71.1 8.1 %scatter_fusion = bf16[128,128,128]{2,1,0:T(8,128)(2,1)} fusion(bf16[128,128,128]{2,1,0:T(8,128)(2,1)} %broadcast_in_dim.28, s32[64]{0:T(128)S(1)} %fusion.38, bf16[64,128,128]{2,1,0:T(8,128)(2,1)S(1)} %get-tuple-element.38), kind=kCustom, calls=%fused_computation.2 | custom fusion | bytes 6291712 | tf_op jit(solution)/shard_map/scatter | solution.py:63
  79.2 0.0 all-to-all-done
  79.2 81.0 %all-to-all-start.1 = ((bf16[32,4,128,128]{3,2,1,0:T(8,128)(2,1)}), bf16[32,4,128,128]{3,2,1,0:T(8,128)(2,1)}, u32[]{:S(2)}, u32[]{:S(2)}) async-start(bf16[32,4,128,128]{3,2,1,0:T(8,128)(2,1)} %bitcast.58), calls=%async_computation.1 | async-start | bytes 8388608 | tf_op jit(solution)/shard_map/all_to_all | solution.py:69
  160.2 0.2 all-gather.5.cloned.1.call-start
  160.4 0.5 all-gather.5.cloned.1.call-update
  161.0 0.6 reduce_max.9
  161.6 0.7 convert_reduce_fusion
  162.3 0.1 and.121
  162.5 0.1 and.113
  162.6 0.1 div.27
  162.7 94.2 %all-to-all-done.1 = bf16[32,4,128,128]{3,2,1,0:T(8,128)(2,1)} async-done(((bf16[32,4,128,128]{3,2,1,0:T(8,128)(2,1)}), bf16[32,4,128,128]{3,2,1,0:T(8,128)(2,1)}, u32[]{:S(2)}, u32[]{:S(2)}) %all-to-all-start.1) | async-done | bytes 4194336 | tf_op jit(solution)/shard_map/all_to_all | solution.py:69
  256.9 5.8 %fusion.7 = bf16[128,128,128]{2,1,0:T(8,128)(2,1)} fusion(bf16[128,128,128]{2,1,0:T(8,128)(2,1)} %bitcast.11, s32[128,128]{1,0:T(8,128)S(1)} %fusion.19), kind=kOutput, calls=%fused_computation.15 | convolution fusion | flops 538968064 | bytes 8454144 | tf_op jit(solution)/shard_map/kis,kiw->ksw/dot_general | solution.py:88
  262.7 7.1 %reshape.165 = bf16[32,4,16384]{2,1,0:T(4,128)(2,1)} reshape(bf16[128,128,128]{2,1,0:T(8,128)(2,1)} %fusion.7) | data formatting | bytes 8388608 | tf_op jit(solution)/shard_map/reshape | solution.py:100
  269.8 6.6 %convolution_convert_fusion = bf16[32,4,16384]{2,1,0:T(4,128)(2,1)} fusion(bf16[32,4,16384]{2,1,0:T(4,128)(2,1)} %reshape.165, s32[32,4]{1,0:T(8,128)S(1)} %get-tuple-element.51, pred[32,4]{1,0:T(8,128)(4,1)S(1)} %broadcast_compare_fusion), kind=kOutput, calls=%fused_computation.13 | convolution fusion | flops 16778752 | bytes 8389248 | tf_op jit(solution)/shard_map/pkj,pjx->pkx/dot_general | solution.py:99
  276.3 6.9 %reshape.166 = bf16[128,16384]{1,0:T(8,128)(2,1)} reshape(bf16[32,4,16384]{2,1,0:T(4,128)(2,1)} %convolution_convert_fusion) | data formatting | bytes 8388608 | tf_op jit(solution)/shard_map/reshape | solution.py:109
  283.2 6.4 %copy.17 = bf16[16384,128]{1,0:T(8,128)(2,1)} copy(bf16[16384,128]{0,1:T(8,128)(2,1)} %bitcast.61) | data formatting | bytes 8388608 | tf_op jit(solution)/shard_map/kt,kx->tx/dot_general | solution.py:109
  289.6 0.0 copy-start.1
  289.6 3.4 %fusion.10 = bf16[128,20,128]{2,1,0:T(8,128)(2,1)S(1)} fusion(bf16[128,128,128]{2,1,0:T(8,128)(2,1)} %bitcast.60, s32[128]{0:T(128)S(1)} %add_select_fusion.2, pred[128]{0:T(512)(128)(4,1)S(1)} %and.121), kind=kOutput, calls=%fused_computation.21 | convolution fusion | flops 84218880 | bytes 4850304 | tf_op jit(solution)/shard_map/kt,kx->tx/dot_general | solution.py:109
  293.0 0.5 copy.18
  293.5 0.0 copy-start.2
  293.5 0.2 copy.19
  293.8 0.0 copy-done.1
  293.8 0.2 fusion.17
  294.0 0.0 all-gather.3.cloned.1.call-done
  294.0 0.0 copy-done
  294.0 3.5 %fusion.12 = bf16[4,128,256]{2,1,0:T(8,128)(2,1)S(1)} fusion(bf16[4,256,256]{2,1,0:T(8,128)(2,1)S(1)} %copy-done, bf16[128,2560,1]{0,1,2:T(8,128)(2,1)S(1)} %bitcast.64, bf16[4,2560,256]{2,1,0:T(8,128)(2,1)} %all-gather.3.cloned.1.call-done), kind=kOutput, calls=%fused_computation.25 | convolution fusion | flops 738459648 | bytes 6684672 | tf_op jit(solution)/shard_map/ebr,erq->ebq/dot_general | solution.py:125
  297.6 0.0 all-gather.5.cloned.1.call-done
  297.6 0.0 copy-done.2
  297.6 4.5 %multiply_reduce_fusion = f32[128,2560]{1,0:T(8,128)S(1)} fusion(bf16[4,128,256]{2,1,0:T(8,128)(2,1)S(1)} %fusion.12, bf16[4,256,2560]{1,2,0:T(8,128)(2,1)} %all-gather.5.cloned.1.call-done, f32[4,2560]{1,0:T(4,128)S(1)} %copy-done.2, f32[4,128]{1,0:T(4,128)S(1)} %fusion.17), kind=kOutput, calls=%fused_computation.16 | convolution fusion | flops 674693120 | bytes 6858752 | tf_op jit(solution)/shard_map/ebr,ern->ebn/dot_general | solution.py:128
  302.1 1.0 fusion.9
  (10 shorter events, 0.2 us)
Async XLA Ops:
  6.5 287.5 %copy-start = (bf16[4,256,256]{2,1,0:T(8,128)(2,1)S(1)}, bf16[4,256,256]{2,1,0:T(8,128)(2,1)}, u32[]{:S(2)}) copy-start(bf16[4,256,256]{2,1,0:T(8,128)(2,1)} %param.22) | copy-start | bytes 1572868
  6.5 287.5 %all-gather.3.cloned.1.call-start = ((), (), s32[]{:S(2)}) async-start(), calls=%async_computation.2 | async-start | bytes 5898240 | tf_op jit(solution)/shard_map/all_gather | solution.py:120
  12.6 66.6 %all-to-all-start = ((s32[32,4,128]{2,1,0:T(4,128)}), s32[32,4,128]{2,1,0:T(4,128)S(1)}, u32[]{:S(2)}, u32[]{:S(2)}) async-start(s32[32,4,128]{2,1,0:T(4,128)} %bitcast.7), calls=%async_computation | async-start | bytes 131072 | tf_op jit(solution)/shard_map/all_to_all | solution.py:76
  79.2 177.7 %all-to-all-start.1 = ((bf16[32,4,128,128]{3,2,1,0:T(8,128)(2,1)}), bf16[32,4,128,128]{3,2,1,0:T(8,128)(2,1)}, u32[]{:S(2)}, u32[]{:S(2)}) async-start(bf16[32,4,128,128]{3,2,1,0:T(8,128)(2,1)} %bitcast.58), calls=%async_computation.1 | async-start | bytes 8388608 | tf_op jit(solution)/shard_map/all_to_all | solution.py:69
  160.2 137.4 %all-gather.5.cloned.1.call-start = ((), (), s32[]{:S(2)}) async-start(), calls=%async_computation.3 | async-start | bytes 5898240 | tf_op jit(solution)/shard_map/all_gather | solution.py:131
  289.6 4.2 %copy-start.1 = (bf16[4,2560]{1,0:T(4,128)(2,1)S(1)}, bf16[4,2560]{1,0:T(4,128)(2,1)}, u32[]{:S(2)}) copy-start(bf16[4,2560]{1,0:T(4,128)(2,1)} %param.25) | copy-start | bytes 61444
  293.5 4.1 %copy-start.2 = (f32[4,2560]{1,0:T(4,128)S(1)}, f32[4,2560]{1,0:T(4,128)}, u32[]{:S(2)}) copy-start(f32[4,2560]{1,0:T(4,128)} %param.24) | copy-start | bytes 122884
Sparse Core Ops, SparseCore 0:
  9.2 40.9 all-gather.2
  162.9 40.3 all-gather.4
where the time goes:
time: 312 us; the launch traced here: 310 us
  waiting for transfers between devices  95.4 us (31%)
  starting transfers between devices  92.5 us (30%)
  local copies, waits for them, and re-layouts  72.1 us (23%)
  matrix products  24 us (8%)
  between operations  14.3 us (5%)
  other arithmetic  11.5 us (4%)
    all_to_all x1, waiting for transfers between devices, on_device(): lax.all_to_all(send_rows.reshape(peers, capacity, block_width, width), 'm...  94.2 us
    all_to_all x1, starting transfers between devices, on_device(): lax.all_to_all(send_rows.reshape(peers, capacity, block_width, width), 'm...  81 us
    gather x3, local copies, waits for them, and re-layouts, pick_rows(): return tables[table_ids[:, None], row_ids]  38.9 us
    all_to_all x1, starting transfers between devices, on_device(): lax.all_to_all(send_code.reshape(peers, capacity, block_width), 'mp', spl...  11.3 us
    scatter x1, local copies, waits for them, and re-layouts, on_device(): send_rows = jnp.zeros((peers * capacity, block_width, width), jnp.bfloat1...  8.07 us
    reshape x1, local copies, waits for them, and re-layouts, on_device(): contrib.reshape(peers, capacity, samples * width)  7.05 us
    reshape x1, local copies, waits for them, and re-layouts, on_device(): rounded.reshape(peers * capacity, samples * width)  6.92 us
    dot_general x1, matrix products, on_device(): jnp.einsum('pkj,pjx->pkx', same.astype(jnp.float32), contrib.reshape(peer...  6.56 us
  transfers between devices with their start and end apart: 4, of which 1 were waited for; matrix products, arithmetic and copies ran while one was open for 33% of the time, Pallas kernels for 0%

commit v1 on v0

v1 whole, which is shorter than its diff:
```python
import functools

import jax
import jax.numpy as jnp
from jax import lax
from jax.experimental import pallas as pl
from jax.experimental.pallas import tpu as pltpu
from jax.sharding import PartitionSpec as P

MESH = pl.DeviceIdType.MESH
CAP = 4
META = 16
RCHUNK = 512


def exchange_kernel(
    peers,
    tab_ref,
    tables_hbm,
    rows_ref,
    slots_ref,
    meta_ref,
    win_hbm,
    wout_hbm,
    recv_hbm,
    win_all,
    wout_all,
    tables_v,
    sbuf,
    table_sem,
    send_sem,
    recv_sem,
    own_sem,
    wsend,
    wrecv,
    wown,
):
    m = lax.axis_index("mp")
    d = lax.axis_index("dp")
    table_count, rows_dev, width = tables_v.shape
    entries = rows_ref.shape[0]
    samples = entries
    y, c = lax.div(d, 2), lax.rem(d, 2)
    up = lax.rem(y + 1, 4) * 2 + c
    dn = lax.rem(y + 3, 4) * 2 + c
    opp = lax.rem(y + 2, 4) * 2 + c
    mate = y * 2 + 1 - c

    table_copy = pltpu.make_async_copy(tables_hbm, tables_v, table_sem)
    table_copy.start()

    def wcopy(src, dst, sem, target):
        return pltpu.make_async_remote_copy(
            src_ref=src,
            dst_ref=dst,
            send_sem=wsend.at[sem],
            recv_sem=wrecv.at[sem],
            device_id={"mp": m, "dp": target},
            device_id_type=MESH,
        )

    pairs = ((win_hbm, win_all), (wout_hbm, wout_all))
    half = win_hbm.shape[0] // 2
    first = []
    for a, (src, dst) in enumerate(pairs):
        for s, target in enumerate((up, dn, mate)):
            first.append(wcopy(src, dst.at[d], a * 8 + s, target))
    for copy in first:
        copy.start()
    own_w = [pltpu.make_async_copy(src, dst.at[d], wown.at[a]) for a, (src, dst) in enumerate(pairs)]
    for copy in own_w:
        copy.start()
    table_copy.wait()

    lane = lax.broadcasted_iota(jnp.int32, (entries, entries), 1).astype(jnp.float32)
    sub = lax.broadcasted_iota(jnp.int32, (samples, entries), 0).astype(jnp.float32)
    wide = lax.broadcasted_iota(jnp.int32, (entries, RCHUNK), 1).astype(jnp.float32)

    def send(step):
        p = lax.rem(m + step, peers)
        return pltpu.make_async_remote_copy(
            src_ref=sbuf.at[p],
            dst_ref=recv_hbm.at[m],
            send_sem=send_sem.at[step],
            recv_sem=recv_sem.at[step],
            device_id={"mp": p, "dp": d},
            device_id_type=MESH,
        )

    def fill(step):
        p = lax.rem(m + step, peers)
        for j in range(CAP):
            slot = p * CAP + j
            column = jnp.sum(
                jnp.where(lane == slot.astype(jnp.float32), rows_ref[...], 0.0), axis=1, keepdims=True
            )
            table = tab_ref[slot]
            picked = jnp.zeros((entries, width), jnp.float32)
            for part in range(rows_dev // RCHUNK):
                hot = jnp.where(column - float(part * RCHUNK) == wide, 1.0, 0.0).astype(jnp.bfloat16)
                picked += jnp.dot(
                    hot,
                    tables_v[table, part * RCHUNK : (part + 1) * RCHUNK, :],
                    preferred_element_type=jnp.float32,
                )
            pool = jnp.where(slots_ref[pl.ds(slot, 1), :] == sub, 1.0, 0.0).astype(jnp.bfloat16)
            pooled = jnp.dot(pool, picked.astype(jnp.bfloat16), preferred_element_type=jnp.float32)
            sbuf[p, j * samples : (j + 1) * samples, :] = pooled.astype(jnp.bfloat16)
        sbuf[p, CAP * samples :, :] = meta_ref[p]

    def body(step, carry):
        fill(step)

        @pl.when(step >= 2)
        def _():
            send(step - 1).start()

        return carry

    lax.fori_loop(1, peers, body, 0)
    fill(jnp.int32(0))
    send(peers - 1).start()
    own = pltpu.make_async_copy(sbuf.at[m], recv_hbm.at[m], own_sem)
    own.start()

    second = []
    for a, (src, dst) in enumerate(pairs):
        wcopy(src, dst.at[dn], a * 8 + 0, up).wait_recv()
        wcopy(src, dst.at[up], a * 8 + 1, dn).wait_recv()
        second.append(wcopy(dst.at[dn, :half], dst.at[dn, :half], a * 8 + 3, up))
        second.append(wcopy(dst.at[up, half:], dst.at[up, half:], a * 8 + 4, dn))
        second.append(wcopy(dst.at[dn], dst.at[dn], a * 8 + 5, mate))
        second.append(wcopy(dst.at[up], dst.at[up], a * 8 + 6, mate))
    for copy in second:
        copy.start()
    third = []
    for a, (src, dst) in enumerate(pairs):
        wcopy(dst.at[opp, :half], dst.at[opp, :half], a * 8 + 3, up).wait_recv()
        wcopy(dst.at[opp, half:], dst.at[opp, half:], a * 8 + 4, dn).wait_recv()
        third.append(wcopy(dst.at[opp], dst.at[opp], a * 8 + 7, mate))
    for copy in third:
        copy.start()
    for a, (src, dst) in enumerate(pairs):
        for s in (2, 5, 6, 7):
            wcopy(src, dst.at[mate], a * 8 + s, mate).wait_recv()
    for copy in first + second + third:
        copy.wait_send()
    for copy in own_w:
        copy.wait()

    def finish(step, carry):
        copy = send(step)
        copy.wait_send()
        q = lax.rem(m + peers - step, peers)
        pltpu.make_async_remote_copy(
            src_ref=sbuf.at[m],
            dst_ref=recv_hbm.at[q],
            send_sem=send_sem.at[step],
            recv_sem=recv_sem.at[step],
            device_id={"mp": q, "dp": d},
            device_id_type=MESH,
        ).wait_recv()
        return carry

    lax.fori_loop(1, peers, finish, 0)
    own.wait()


def exchange(tables, tab_slot, rows_t, slot_code, meta, cross_in, cross_out, peers):
    table_count, rows_dev, width = tables.shape
    entries = rows_t.shape[0]
    dp = lax.axis_size("dp")
    packed = CAP * entries + META
    hbm = pl.BlockSpec(memory_space=pl.ANY)
    vmem = pl.BlockSpec(memory_space=pltpu.VMEM)
    return pl.pallas_call(
        functools.partial(exchange_kernel, peers),
        out_shape=(
            jax.ShapeDtypeStruct((peers, packed, width), jnp.bfloat16),
            jax.ShapeDtypeStruct((dp,) + cross_in.shape, jnp.bfloat16),
            jax.ShapeDtypeStruct((dp,) + cross_out.shape, jnp.bfloat16),
        ),
        in_specs=[pl.BlockSpec(memory_space=pltpu.SMEM), hbm, vmem, vmem, vmem, hbm, hbm],
        out_specs=(hbm, hbm, hbm),
        scratch_shapes=[
            pltpu.VMEM((table_count, rows_dev, width), jnp.bfloat16),
            pltpu.VMEM((peers, packed, width), jnp.bfloat16),
            pltpu.SemaphoreType.DMA,
            pltpu.SemaphoreType.DMA((peers,)),
            pltpu.SemaphoreType.DMA((peers,)),
            pltpu.SemaphoreType.DMA,
            pltpu.SemaphoreType.DMA((16,)),
            pltpu.SemaphoreType.DMA((16,)),
            pltpu.SemaphoreType.DMA((2,)),
        ],
        compiler_params=pltpu.CompilerParams(has_side_effects=True, vmem_limit_bytes=60 * 1024 * 1024),
        name="exchange",
    )(tab_slot, tables, rows_t, slot_code, meta, cross_in, cross_out)


def cross_kernel(
    tab_ref,
    recv_ref,
    mix_ref,
    bias_ref,
    gate_ref,
    win_hbm,
    wout_hbm,
    out_ref,
    acc,
    win_v,
    wout_v,
    sems,
):
    peers = recv_ref.shape[0]
    samples, wide = acc.shape
    width = recv_ref.shape[2]
    dp, experts, cols, rank = win_v.shape
    in_copy = pltpu.make_async_copy(win_hbm, win_v, sems.at[0])
    out_copy = pltpu.make_async_copy(wout_hbm, wout_v, sems.at[1])
    in_copy.start()
    out_copy.start()
    acc[...] = jnp.zeros_like(acc)

    def add(q, carry):
        for j in range(CAP):
            table = tab_ref[q, j] - 1

            @pl.when(table >= 0)
            def _():
                col = pl.ds(pl.multiple_of(table * width, width), width)
                acc[:, col] += recv_ref[q, j * samples : (j + 1) * samples, :].astype(jnp.float32)

        return carry

    lax.fori_loop(0, peers, add, 0)
    embedded = acc[...].astype(jnp.bfloat16)
    gate = jax.nn.sigmoid(
        lax.dot_general(embedded, gate_ref[...], (((1,), (1,)), ((), ())), preferred_element_type=jnp.float32)
    )
    in_copy.wait()
    mixed = []
    for e in range(experts):
        projected = jnp.zeros((samples, rank), jnp.float32)
        for k in range(dp):
            projected += jnp.dot(
                embedded[:, k * cols : (k + 1) * cols], win_v[k, e], preferred_element_type=jnp.float32
            )
        hidden = jnp.tanh(projected).astype(jnp.bfloat16)
        mixed.append(
            jnp.tanh(jnp.dot(hidden, mix_ref[e], preferred_element_type=jnp.float32)).astype(jnp.bfloat16)
        )
    out_copy.wait()
    for k in range(dp):
        span = slice(k * cols, (k + 1) * cols)
        weighted = jnp.zeros((samples, cols), jnp.float32)
        for e in range(experts):
            grown = jnp.dot(mixed[e], wout_v[k, e], preferred_element_type=jnp.float32)
            weighted += gate[:, e : e + 1] * (grown + bias_ref[e : e + 1, span])
        base = embedded[:, span].astype(jnp.float32)
        out_ref[:, span] = (base + base * weighted).astype(jnp.bfloat16)


def cross(recv, tabs, win_all, wout_all, cross_mix, cross_bias, gate_weight):
    peers, packed, width = recv.shape
    samples = (packed - META) // CAP
    wide = cross_bias.shape[1]
    hbm = pl.BlockSpec(memory_space=pl.ANY)
    vmem = pl.BlockSpec(memory_space=pltpu.VMEM)
    return pl.pallas_call(
        cross_kernel,
        out_shape=jax.ShapeDtypeStruct((samples, wide), jnp.bfloat16),
        in_specs=[pl.BlockSpec(memory_space=pltpu.SMEM), vmem, vmem, vmem, vmem, hbm, hbm],
        out_specs=vmem,
        scratch_shapes=[
            pltpu.VMEM((samples, wide), jnp.float32),
            pltpu.VMEM(win_all.shape, jnp.bfloat16),
            pltpu.VMEM(wout_all.shape, jnp.bfloat16),
            pltpu.SemaphoreType.DMA((2,)),
        ],
        compiler_params=pltpu.CompilerParams(vmem_limit_bytes=60 * 1024 * 1024),
        name="cross",
    )(tabs, recv, cross_mix, cross_bias, gate_weight, win_all, wout_all)


def on_device(
    tables,
    block_rows,
    block_slots,
    block_table,
    block_peer,
    block_len,
    block_count,
    cross_in,
    cross_mix,
    cross_out,
    cross_bias,
    gate_weight,
):
    peers = lax.axis_size("mp")
    blocks, entries = block_rows.shape
    ids = jnp.arange(blocks, dtype=jnp.int32)
    live = ids < block_count[0]
    peer = block_peer[:, 0]
    earlier = (peer[:, None] == peer[None, :]) & (ids[None, :] < ids[:, None])
    position = jnp.sum(earlier.astype(jnp.int32), axis=1)
    target = jnp.where(live, peer * CAP + position, -1)
    pick = target[None, :] == jnp.arange(peers * CAP, dtype=jnp.int32)[:, None]
    tab_code = jnp.sum(jnp.where(pick, block_table[None, :] + 1, 0), axis=1)
    live_entry = jnp.arange(entries, dtype=jnp.int32)[None, :] < block_len[:, None]
    row_code = jnp.where(live_entry, block_rows + 1, 0)
    slot_code = jnp.where(live_entry, block_slots + 1, 0)
    rows_t = jnp.sum(jnp.where(pick.T[:, None, :], row_code[:, :, None], 0), axis=0) - 1
    slots_s = jnp.sum(jnp.where(pick[:, :, None], slot_code[None, :, :], 0), axis=1) - 1
    meta = jnp.pad(
        tab_code.reshape(peers, 1, CAP).astype(jnp.bfloat16), ((0, 0), (0, META - 1), (0, tables.shape[2] - CAP))
    )
    recv, win_all, wout_all = exchange(
        tables,
        jnp.maximum(tab_code - 1, 0),
        rows_t.astype(jnp.float32),
        slots_s.astype(jnp.float32),
        meta,
        cross_in,
        cross_out,
        peers,
    )
    tabs = recv[:, CAP * B_DEV, :CAP].astype(jnp.int32)
    return cross(recv, tabs, win_all, wout_all, cross_mix, cross_bias, gate_weight)


B_DEV = 128


def solution(mesh):
    in_specs = (
        P(None, "mp", None),
        P(("mp", "dp"), None),
        P(("mp", "dp"), None),
        P(("mp", "dp")),
        P(("mp", "dp"), None),
        P(("mp", "dp")),
        P(("mp", "dp")),
        P(None, "dp", None),
        P(),
        P(None, None, "dp"),
        P(),
        P(),
    )
    out_specs = P(("mp", "dp"), None)
    return jax.shard_map(
        on_device, mesh=mesh, in_specs=in_specs, out_specs=out_specs, check_vma=False
    )
```

time: 312 us -> 156 us (0.50)
  the two profiles are of different devices: /device:TPU:8 before, /device:TPU:161 now
where the time goes in v1:
time: 156 us
  Pallas kernels  143 us (92%)
  other arithmetic  8.91 us (6%)
  local copies, waits for them, and re-layouts  3.19 us (2%)
    pallas_call x1, Pallas kernels, exchange(): pl.pallas_call(functools.partial(exchange_kernel, peers), out_shape=(jax....  133 us
    pallas_call x1, Pallas kernels, cross(): pl.pallas_call(cross_kernel, out_shape=jax.ShapeDtypeStruct((samples, wid...  10.2 us

profile of v1, /device:TPU:161, one launch (start us, length us, event | category | flops | bytes accessed | tf_op | source)
XLA Modules:
  0.0 155.9 jit_solution(14628838388257021240)
XLA Ops:
  0.7 0.9 convert_reduce_fusion
  1.6 0.7 compare_select_fusion
  2.2 0.1 select_reduce_fusion.2
  2.3 0.5 fusion.1
  2.9 0.1 iota_compare_fusion.1
  2.9 0.1 iota_compare_fusion.2
  3.0 0.1 copy.26
  3.1 0.1 convert_element_type.38
  3.3 0.9 add_select_fusion
  4.2 1.6 %select_reduce_fusion = s32[128,128]{1,0:T(8,128)S(1)} fusion(s32[64,128]{1,0:T(8,128)S(1)} %get-tuple-element.13, pred[128,64]{1,0:T(8,128)(4,1)S(1)} %copy.26), kind=kLoop, calls=%fused_computation | loop fusion | flops 2080768 | bytes 106496 | tf_op jit(solution)/shard_map/reduce_sum | solution.py:314
  5.8 0.6 add_convert_fusion.slots_ref
  6.4 1.4 select_reduce_fusion.1
  7.8 0.6 add_convert_fusion.1.rows_ref
  8.4 0.7 pad.4.meta_ref
  9.1 2.3 %copy.28.wout_hbm = bf16[4,256,320]{2,1,0:T(8,128)(2,1)} copy(bf16[4,256,320]{1,2,0:T(8,128)(2,1)} %param.21) | data formatting | bytes 1310720 | tf_op args[9]
  11.3 132.9 %exchange.1 = (bf16[32,528,128]{2,1,0:T(8,128)(2,1)}, bf16[8,4,320,256]{3,2,1,0:T(8,128)(2,1)}, bf16[8,4,256,320]{3,2,1,0:T(8,128)(2,1)}) custom-call(s32[128]{0:T(128)} %get-tuple-element.12.tab_ref, bf16[20,2048,128]{2,1,0:T(8,128)(2,1)} %tables_hbm.1, f32[128,128]{1,0:T(8,128)} %add_convert_fusion.1.rows_ref, f32[128,128]{1,0:T(8,128)} %add_convert_fusion.slots_ref, ...), custom_call_target="tpu_custom_call" | custom-call | tf_op jit(solution)/shard_map/exchange/pallas_call | solution.py:176
  144.2 1.5 slice_convert_fusion
  145.7 10.2 %cross.1 = bf16[128,2560]{1,0:T(8,128)(2,1)} custom-call(s32[32,4]{1,0:T(8,128)} %bitcast.5, bf16[32,528,128]{2,1,0:T(8,128)(2,1)} %get-tuple-element.8.recv_ref, bf16[4,256,256]{2,1,0:T(8,128)(2,1)} %mix_ref.1, f32[4,2560]{1,0:T(4,128)} %bias_ref.1, bf16[4,2560]{1,0:T(4,128)(2,1)} %gate_ref.1, bf16[8,4,320,256]{3,2,1,0:T(8,128)(2,1)} %get-tuple-element.9.win_hbm, ...), custom_call_target="tpu_custom_call" | custom-call | tf_op jit(solution)/shard_map/cross/pallas_call | solution.py:270

commit v2 on v0

v2 whole, which is shorter than its diff:
```python
import functools

import jax
import jax.numpy as jnp
from jax import lax
from jax.experimental import pallas as pl
from jax.experimental.pallas import tpu as pltpu
from jax.sharding import PartitionSpec as P

MESH = pl.DeviceIdType.MESH
F32, BF16 = jnp.float32, jnp.bfloat16
CAP = 4
META = 8
TIGHT = 320
RCHUNK = 512
LIMIT = 60 * 1024 * 1024


def iota(shape, axis):
    return lax.broadcasted_iota(jnp.int32, shape, axis).astype(F32)


def dot(a, b):
    return jnp.dot(a, b, preferred_element_type=F32)


def dot_t(a, b):
    return lax.dot_general(a, b, (((1,), (1,)), ((), ())), preferred_element_type=F32)


def dot_l(a, b):
    return lax.dot_general(a, b, (((0,), (0,)), ((), ())), preferred_element_type=F32)


def hot(mask):
    return jnp.where(mask, 1.0, 0.0).astype(BF16)


def prep_kernel(
    tight, count_ref, rows_ref, slots_ref, table_ref, peer_ref, len_ref, tab_o, rows_o, slots_o, qh_o, ql_o, meta_o, need_o, used
):
    blocks, entries = rows_ref.shape
    slots_n = rows_o.shape[1]
    count = count_ref[0].astype(F32)
    k_sub, k_lane = iota((blocks, blocks), 0), iota((blocks, blocks), 1)
    eye = k_sub == k_lane

    def column(row):
        return jnp.sum(jnp.where(eye, row, 0.0), axis=1, keepdims=True)

    table_r, peer_r = table_ref[...].astype(F32), peer_ref[...].astype(F32)
    table_c, peer_c, len_c = column(table_r), column(peer_r), column(len_ref[...].astype(F32))
    live_r, live_c = k_lane[:1] < count, k_sub[:, :1] < count
    same = peer_c == peer_r
    before = same & (k_lane < k_sub)
    alike = same & (column(table_r) == table_r) & live_r & live_c
    follows_c = jnp.max(jnp.where(alike & (k_lane < k_sub), 1.0, 0.0), axis=1, keepdims=True)
    follows_r = jnp.max(jnp.where(alike & (k_sub < k_lane), 1.0, 0.0), axis=0, keepdims=True)
    leads_c = jnp.where(live_c, 1.0 - follows_c, 0.0)
    pos_c = jnp.sum(jnp.where(before, 1.0, 0.0), axis=1, keepdims=True)
    pos_r = jnp.sum(jnp.where(same & (k_sub < k_lane), 1.0, 0.0), axis=0, keepdims=True)
    target_r = jnp.where(live_r, peer_r * CAP + pos_r, -1.0)
    target_c = jnp.where(live_c, peer_c * CAP + pos_c, -1.0)
    place = hot(iota((slots_n, blocks), 0) == target_r)
    place_t = hot(target_c == iota((blocks, slots_n), 1))

    live_entry = (iota((blocks, entries), 1) < len_c) & live_c
    slot_code = jnp.where(live_entry, slots_ref[...].astype(F32) + 1.0, 0.0)
    slots_o[...] = dot(place, slot_code.astype(BF16)) - 1.0
    row_code = jnp.where(live_entry, rows_ref[...].astype(F32) + 1.0, 0.0)
    high = jnp.floor(row_code * (1.0 / 64.0))
    low = row_code - 64.0 * high
    rows_o[...] = 64.0 * dot_l(high.astype(BF16), place_t) + dot_l(low.astype(BF16), place_t) - 1.0
    tab_o[...] = dot(jnp.broadcast_to(table_r, (8, blocks)).astype(BF16), place_t).astype(jnp.int32)

    lanes = iota((entries, entries), 1)
    if tight:
        slot_t = slot_code.T - 1.0
        for k in range(blocks):
            touched = jnp.where(slot_t[:, k : k + 1] == lanes, 1.0, 0.0)
            used[k : k + 1, :] = jnp.minimum(jnp.sum(touched, axis=0, keepdims=True), 1.0)
        taken = leads_c * jnp.minimum(dot(hot(alike), used[...].astype(BF16)), 1.0)
    else:
        taken = leads_c + jnp.zeros((blocks, entries), F32)
    rank = dot(taken.astype(BF16), hot(iota((entries, entries), 0) < lanes))
    amount_c = jnp.sum(taken, axis=1, keepdims=True)
    amount_r = jnp.sum(jnp.where(eye, amount_c, 0.0), axis=0, keepdims=True)
    off_c = jnp.sum(jnp.where(before, amount_r, 0.0), axis=1, keepdims=True)
    need_o[...] = jnp.zeros_like(need_o) + jnp.max(jnp.where(live_c, off_c + amount_c, 0.0))

    spot = jnp.where(taken > 0.0, off_c + rank + 1.0, 0.0)
    spot_high = jnp.floor(spot * (1.0 / 64.0))
    spot_low = spot - 64.0 * spot_high
    led = hot(alike & (follows_r == 0.0))
    qh_o[...] = dot(place, dot(led, spot_high.astype(BF16)).astype(BF16))
    ql_o[...] = dot(place, dot(led, spot_low.astype(BF16)).astype(BF16))

    off_high = jnp.floor(off_c * (1.0 / 16.0))
    lane_e = iota((blocks, entries), 1)
    facts = jnp.where(lane_e == 0.0, table_c + 1.0, jnp.where(lane_e == 1.0, off_high, off_c - 16.0 * off_high))
    facts = jnp.where(lane_e < 3.0, leads_c * facts, 0.0)
    line = lax.broadcasted_iota(jnp.int32, (meta_o.shape[0], blocks), 0)
    pair, part = (line >> 3) * CAP, line & 7
    rank_line = hot(jnp.where(part < CAP, pair + part, -2).astype(F32) == target_r)
    fact_line = hot(jnp.where((part >= CAP) & (part < 2 * CAP), pair + part - CAP, -2).astype(F32) == target_r)
    meta = dot(rank_line, (taken * (rank + 1.0)).astype(BF16)) + dot(fact_line, facts.astype(BF16))
    meta_o[...] = meta.astype(BF16)


def prep(tight, peers, count, rows, slots, table, peer, length):
    blocks, entries = rows.shape
    slots_n = peers * CAP
    vmem = pl.BlockSpec(memory_space=pltpu.VMEM)
    return pl.pallas_call(
        functools.partial(prep_kernel, tight),
        out_shape=(
            jax.ShapeDtypeStruct((8, slots_n), jnp.int32),
            jax.ShapeDtypeStruct((entries, slots_n), F32),
            jax.ShapeDtypeStruct((slots_n, entries), F32),
            jax.ShapeDtypeStruct((slots_n, entries), F32),
            jax.ShapeDtypeStruct((slots_n, entries), F32),
            jax.ShapeDtypeStruct((peers * META, entries), BF16),
            jax.ShapeDtypeStruct((8, entries), F32),
        ),
        in_specs=[pl.BlockSpec(memory_space=pltpu.SMEM)] + [vmem] * 5,
        out_specs=(vmem,) * 7,
        scratch_shapes=[pltpu.VMEM((blocks, entries), F32)],
        name="prep_tight" if tight else "prep_full",
    )(count, rows, slots, table, peer, length)


def exchange_kernel(tight, peers, *refs):
    if tight:
        (tab_ref, tables_hbm, rows_ref, slots_ref, qh_ref, ql_ref, meta_ref, need_ref, win_hbm, wout_hbm) = refs[:10]
        (got_ref, facts_ref, flag_ref, win_all, wout_all) = refs[10:15]
        (tables_v, sbuf, rbuf, table_sem, send_sem, recv_sem) = refs[15:21]
        (mp_need, dp_need, mine, nsend, nrecv, dsend, drecv, wsend, wrecv, wown) = refs[21:]
    else:
        (tab_ref, tables_hbm, rows_ref, slots_ref, qh_ref, ql_ref, meta_ref) = refs[:7]
        (got_ref, facts_ref) = refs[7:9]
        (tables_v, sbuf, rbuf, table_sem, send_sem, recv_sem) = refs[9:]
    m = lax.axis_index("mp")
    d = lax.axis_index("dp")
    table_count, rows_dev, width = tables_v.shape
    entries = rows_ref.shape[0]
    samples = entries
    space = sbuf.shape[1] - META
    x, z = lax.div(m, 8), lax.rem(m, 8)
    self_step = 28

    def shift(step):
        turn = lax.div(step, 4)
        half = lax.div(turn, 2)
        dz = jnp.where(lax.rem(turn, 2) == 0, 4 + half, 3 - half)
        return lax.rem(step, 4), dz

    def ahead(step):
        dx, dz = shift(step)
        return lax.rem(x + dx, 4) * 8 + lax.rem(z + dz, 8)

    def behind(step):
        dx, dz = shift(step)
        return lax.rem(x + 4 - dx, 4) * 8 + lax.rem(z + 8 - dz, 8)

    table_copy = pltpu.make_async_copy(tables_hbm, tables_v, table_sem)
    table_copy.start()

    barrier = pltpu.get_barrier_semaphore()

    def greet(step, carry):
        pl.semaphore_signal(
            barrier, inc=1, device_id={"mp": lax.rem(m + step, peers), "dp": d}, device_id_type=MESH
        )
        return carry

    lax.fori_loop(1, peers, greet, 0)
    if tight:
        for step in range(1, 8):
            pl.semaphore_signal(
                barrier, inc=1, device_id={"mp": m, "dp": lax.rem(d + step, 8)}, device_id_type=MESH
            )
        pl.semaphore_wait(barrier, peers - 1 + 7)
    else:
        pl.semaphore_wait(barrier, peers - 1)

    if tight:
        y, c = lax.div(d, 2), lax.rem(d, 2)
        up = lax.rem(y + 1, 4) * 2 + c
        dn = lax.rem(y + 3, 4) * 2 + c
        opp = lax.rem(y + 2, 4) * 2 + c
        mate = y * 2 + 1 - c
        cols = win_hbm.shape[1]
        half = win_hbm.shape[0] // 2
        pairs = ((win_hbm, win_all), (wout_hbm, wout_all))

        def part(ref, owner, lead=slice(None)):
            return ref.at[lead, pl.ds(pl.multiple_of(owner * cols, cols), cols), :]

        def wcopy(src, dst, sem, target):
            return pltpu.make_async_remote_copy(
                src_ref=src,
                dst_ref=dst,
                send_sem=wsend.at[sem],
                recv_sem=wrecv.at[sem],
                device_id={"mp": m, "dp": target},
                device_id_type=MESH,
            )

        first = [
            wcopy(src, part(dst, d), a * 8 + s, target)
            for a, (src, dst) in enumerate(pairs)
            for s, target in enumerate((up, dn, mate))
        ]
        for copy in first:
            copy.start()
        own_w = [
            pltpu.make_async_copy(src, part(dst, d), wown.at[a]) for a, (src, dst) in enumerate(pairs)
        ]
        for copy in own_w:
            copy.start()

        def need_copy(step):
            return pltpu.make_async_remote_copy(
                src_ref=need_ref,
                dst_ref=mp_need.at[step],
                send_sem=nsend.at[step],
                recv_sem=nrecv.at[step],
                device_id={"mp": lax.rem(m + step, peers), "dp": d},
                device_id_type=MESH,
            )

        def tell(step, carry):
            need_copy(step).start()
            return carry

        lax.fori_loop(1, peers, tell, 0)
    table_copy.wait()

    lane = iota((entries, entries), 1)
    sub = iota((samples, entries), 0)
    wide = iota((entries, RCHUNK), 1)
    deep = iota((space, entries), 0)
    first_row = iota((8, samples), 0) == 0.0
    long = iota((samples, space), 1)

    def send(step):
        return pltpu.make_async_remote_copy(
            src_ref=sbuf.at[step],
            dst_ref=rbuf.at[step],
            send_sem=send_sem.at[step],
            recv_sem=recv_sem.at[step],
            device_id={"mp": ahead(step), "dp": d},
            device_id_type=MESH,
        )

    def fill(step):
        p = ahead(step)
        spread, gathered = [], []
        for j in range(CAP):
            slot = p * CAP + j
            column = jnp.sum(jnp.where(lane == slot.astype(F32), rows_ref[...], 0.0), axis=1, keepdims=True)
            table = tab_ref[0, slot]
            picked = jnp.zeros((entries, width), F32)
            for piece in range(rows_dev // RCHUNK):
                picked += dot(
                    hot(column - float(piece * RCHUNK) == wide),
                    tables_v[table, piece * RCHUNK : (piece + 1) * RCHUNK, :],
                )
            gathered.append(picked.astype(BF16))
            halves = jnp.where(first_row, qh_ref[pl.ds(slot, 1), :], ql_ref[pl.ds(slot, 1), :]).astype(BF16)
            found = dot(halves, hot(slots_ref[pl.ds(slot, 1), :] == sub))
            spread.append(hot(64.0 * found[0:1] + found[1:2] - 1.0 == deep))
        packed = dot(jnp.concatenate(spread, axis=1), jnp.concatenate(gathered, axis=0))
        sbuf[step, :space, :] = packed.astype(BF16)
        sbuf[step, space:, :] = meta_ref[p]

    def body(step, carry):
        fill(step)
        last = step - 1

        @pl.when((step >= 1) & (last != self_step))
        def _():
            send(last).start()

        return carry

    lax.fori_loop(0, peers, body, 0)

    if tight:
        def hear(step, carry):
            need_copy(step).wait_recv()
            return jnp.maximum(carry, mp_need[step])

        mine[...] = lax.fori_loop(1, peers, hear, need_ref[...])

    send(peers - 1).start()

    if tight:

        def flag_copy(step):
            return pltpu.make_async_remote_copy(
                src_ref=mine,
                dst_ref=dp_need.at[step],
                send_sem=dsend.at[step],
                recv_sem=drecv.at[step],
                device_id={"mp": m, "dp": lax.rem(d + step, 8)},
                device_id_type=MESH,
            )

        for step in range(1, 8):
            flag_copy(step).start()

        low, high = slice(0, half), slice(half, 2 * half)
        second = []
        for a, (src, dst) in enumerate(pairs):
            wcopy(src, part(dst, dn), a * 8 + 0, up).wait_recv()
            wcopy(src, part(dst, up), a * 8 + 1, dn).wait_recv()
            second.append(wcopy(part(dst, dn, low), part(dst, dn, low), a * 8 + 3, up))
            second.append(wcopy(part(dst, up, high), part(dst, up, high), a * 8 + 4, dn))
            second.append(wcopy(part(dst, dn), part(dst, dn), a * 8 + 5, mate))
            second.append(wcopy(part(dst, up), part(dst, up), a * 8 + 6, mate))
        for copy in second:
            copy.start()

    def unpack(buf, source, index):
        facts = buf[index, space:, :].astype(F32)[: 2 * CAP]
        facts_ref[source] = facts
        turned = facts.T
        spots = []
        for j in range(CAP):
            code = turned[:, j : j + 1]
            offset = 16.0 * turned[1:2, CAP + j : CAP + j + 1] + turned[2:3, CAP + j : CAP + j + 1]
            spots.append(hot(jnp.where(code > 0.0, code - 1.0 + offset, -1.0) == long))
        got = dot(jnp.concatenate(spots, axis=0), buf[index, :space, :])
        got_ref[source] = got.astype(BF16)

    unpack(sbuf, m, self_step)

    def take(step, carry):
        @pl.when(step != self_step)
        def _():
            pltpu.make_async_remote_copy(
                src_ref=sbuf.at[step],
                dst_ref=rbuf.at[step],
                send_sem=send_sem.at[step],
                recv_sem=recv_sem.at[step],
                device_id={"mp": behind(step), "dp": d},
                device_id_type=MESH,
            ).wait_recv()
            unpack(rbuf, behind(step), step)

        return carry

    if tight:
        lax.fori_loop(0, peers // 2, take, 0)
        third = []
        for a, (src, dst) in enumerate(pairs):
            wcopy(part(dst, opp, low), part(dst, opp, low), a * 8 + 3, up).wait_recv()
            wcopy(part(dst, opp, high), part(dst, opp, high), a * 8 + 4, dn).wait_recv()
            third.append(wcopy(part(dst, opp), part(dst, opp), a * 8 + 7, mate))
        for copy in third:
            copy.start()
        lax.fori_loop(peers // 2, peers, take, 0)
        worst = mine[...]
        for step in range(1, 8):
            flag_copy(step).wait()
            worst = jnp.maximum(worst, dp_need[step])
        flag_ref[...] = worst
        for a, (src, dst) in enumerate(pairs):
            for s in (2, 5, 6, 7):
                wcopy(src, part(dst, mate), a * 8 + s, mate).wait_recv()
        for copy in first + second + third:
            copy.wait_send()
        for copy in own_w:
            copy.wait()

        def told(step, carry):
            need_copy(step).wait_send()
            return carry

        lax.fori_loop(1, peers, told, 0)
    else:
        lax.fori_loop(0, peers, take, 0)

    def sent(step, carry):
        @pl.when(step != self_step)
        def _():
            send(step).wait_send()

        return carry

    lax.fori_loop(0, peers, sent, 0)


def exchange(tight, peers, tables, prepared, weights):
    tab, rows_t, slots_s, q_high, q_low, meta, need = prepared
    table_count, rows_dev, width = tables.shape
    entries, slots_n = rows_t.shape
    space = TIGHT if tight else CAP * entries
    hbm = pl.BlockSpec(memory_space=pl.ANY)
    vmem = pl.BlockSpec(memory_space=pltpu.VMEM)
    sems = pltpu.SemaphoreType.DMA
    operands = [tab, tables, rows_t, slots_s, q_high, q_low, meta.reshape(peers, META, width)]
    in_specs = [pl.BlockSpec(memory_space=pltpu.SMEM), hbm, vmem, vmem, vmem, vmem, vmem]
    out_shape = [
        jax.ShapeDtypeStruct((peers, CAP * entries, width), BF16),
        jax.ShapeDtypeStruct((peers, 2 * CAP, width), F32),
    ]
    out_specs = [vmem, vmem]
    scratch = [
        pltpu.VMEM((table_count, rows_dev, width), BF16),
        pltpu.VMEM((peers, space + META, width), BF16),
        pltpu.VMEM((peers, space + META, width), BF16),
        sems,
        sems((peers,)),
        sems((peers,)),
    ]
    if tight:
        operands += [need, *weights]
        in_specs += [vmem, hbm, hbm]
        out_shape.append(jax.ShapeDtypeStruct(need.shape, F32))
        out_specs.append(vmem)
        for w in weights:
            experts, cols, rank = w.shape
            out_shape.append(jax.ShapeDtypeStruct((experts, cols * lax.axis_size("dp"), rank), BF16))
            out_specs.append(hbm)
        scratch += [
            pltpu.VMEM((peers,) + need.shape, F32),
            pltpu.VMEM((8,) + need.shape, F32),
            pltpu.VMEM(need.shape, F32),
            sems((peers,)),
            sems((peers,)),
            sems((8,)),
            sems((8,)),
            sems((16,)),
            sems((16,)),
            sems((2,)),
        ]
    return pl.pallas_call(
        functools.partial(exchange_kernel, tight, peers),
        out_shape=out_shape,
        in_specs=in_specs,
        out_specs=out_specs,
        scratch_shapes=scratch,
        compiler_params=pltpu.CompilerParams(
            has_side_effects=True, collective_id=0 if tight else 1, vmem_limit_bytes=LIMIT
        ),
        name="exchange_tight" if tight else "exchange_full",
    )(*operands)


def cross_kernel(
    tab_ref, got_ref, mix_ref, bias_ref, gate_ref, win_hbm, wout_hbm, out_ref, acc, win_v, wout_v, sems
):
    peers = got_ref.shape[0]
    samples, wide = acc.shape
    width = got_ref.shape[2]
    experts = win_v.shape[0]
    in_copy = pltpu.make_async_copy(win_hbm, win_v, sems.at[0])
    out_copy = pltpu.make_async_copy(wout_hbm, wout_v, sems.at[1])
    in_copy.start()
    out_copy.start()
    acc[...] = jnp.zeros_like(acc)

    def add(q, carry):
        for j in range(CAP):
            table = tab_ref[q, j] - 1

            @pl.when(table >= 0)
            def _():
                col = pl.ds(pl.multiple_of(table * width, width), width)
                acc[:, col] += got_ref[q, j * samples : (j + 1) * samples, :].astype(F32)

        return carry

    lax.fori_loop(0, peers, add, 0)
    embedded = acc[...].astype(BF16)
    gate = jax.nn.sigmoid(dot_t(embedded, gate_ref[...]))
    in_copy.wait()
    mixed = []
    for e in range(experts):
        hidden = jnp.tanh(dot(embedded, win_v[e])).astype(BF16)
        mixed.append(jnp.tanh(dot(hidden, mix_ref[e])).astype(BF16))
    out_copy.wait()
    span_cols = 512
    for k in range(wide // span_cols):
        span = slice(k * span_cols, (k + 1) * span_cols)
        weighted = jnp.zeros((samples, span_cols), F32)
        for e in range(experts):
            grown = dot_t(mixed[e], wout_v[e, span, :])
            weighted += gate[:, e : e + 1] * (grown + bias_ref[e : e + 1, span])
        base = embedded[:, span].astype(F32)
        out_ref[:, span] = (base + base * weighted).astype(BF16)


def cross(tabs, got, win_all, wout_all, cross_mix, cross_bias, gate_weight):
    samples = got.shape[1] // CAP
    wide = cross_bias.shape[1]
    hbm = pl.BlockSpec(memory_space=pl.ANY)
    vmem = pl.BlockSpec(memory_space=pltpu.VMEM)
    return pl.pallas_call(
        cross_kernel,
        out_shape=jax.ShapeDtypeStruct((samples, wide), BF16),
        in_specs=[pl.BlockSpec(memory_space=pltpu.SMEM), vmem, vmem, vmem, vmem, hbm, hbm],
        out_specs=vmem,
        scratch_shapes=[
            pltpu.VMEM((samples, wide), F32),
            pltpu.VMEM(win_all.shape, BF16),
            pltpu.VMEM(wout_all.shape, BF16),
            pltpu.SemaphoreType.DMA((2,)),
        ],
        compiler_params=pltpu.CompilerParams(vmem_limit_bytes=LIMIT),
        name="cross",
    )(tabs, got, cross_mix, cross_bias, gate_weight, win_all, wout_all)


def on_device(
    tables,
    block_rows,
    block_slots,
    block_table,
    block_peer,
    block_len,
    block_count,
    cross_in,
    cross_mix,
    cross_out,
    cross_bias,
    gate_weight,
):
    peers = lax.axis_size("mp")
    blocks = block_rows.shape[0]
    inputs = (
        block_count,
        block_rows,
        block_slots,
        block_table.reshape(1, blocks),
        block_peer.reshape(1, blocks),
        block_len.reshape(1, blocks),
    )
    prepared = prep(True, peers, *inputs)
    got, facts, flag, win_all, wout_all = exchange(
        True, peers, tables, prepared, (cross_in, cross_out.transpose(0, 2, 1))
    )

    def full():
        return tuple(exchange(False, peers, tables, prep(False, peers, *inputs), ()))

    got, facts = lax.cond(flag[0, 0] > TIGHT, full, lambda: (got, facts))
    tabs = facts[:, CAP:, 0].astype(jnp.int32)
    return cross(tabs, got, win_all, wout_all, cross_mix, cross_bias, gate_weight)


def solution(mesh):
    in_specs = (
        P(None, "mp", None),
        P(("mp", "dp"), None),
        P(("mp", "dp"), None),
        P(("mp", "dp")),
        P(("mp", "dp"), None),
        P(("mp", "dp")),
        P(("mp", "dp")),
        P(None, "dp", None),
        P(),
        P(None, None, "dp"),
        P(),
        P(),
    )
    out_specs = P(("mp", "dp"), None)
    return jax.shard_map(
        on_device, mesh=mesh, in_specs=in_specs, out_specs=out_specs, check_vma=False
    )
```

time: 312 us -> 102 us (0.33)
  Pallas kernels: 0 us -> 96.8 us
  waiting for transfers between devices: 95.4 us -> 0 us
  starting transfers between devices: 92.5 us -> 0 us
  local copies, waits for them, and re-layouts: 72.1 us -> 2.14 us
  matrix products: 24 us -> 0 us
  between operations: 14.3 us -> 1.4 us
  other arithmetic: 11.5 us -> 0.01 us
    pallas_call x0 -> x3, Pallas kernels: none -> 96.8 us  [the longest x1 83.5 us: exchange(): pl.pallas_call(functools.partial(exchange_kernel, tight, peers), out_shap...]
    all_to_all x2 -> x0, waiting for transfers between devices: 94.2 us -> none  [the longest x1 94.2 us: on_device(): lax.all_to_all(send_rows.reshape(peers, capacity, block_width, width), 'm...]
    all_to_all x2 -> x0, starting transfers between devices: 92.3 us -> none  [the longest x1 81 us: on_device(): lax.all_to_all(send_rows.reshape(peers, capacity, block_width, width), 'm...]
    gather x3 -> x0, local copies, waits for them, and re-layouts: 38.9 us -> none  [pick_rows(): return tables[table_ids[:, None], row_ids]]
    dot_general x6 -> x0, matrix products: 24 us -> none  [the longest x1 6.56 us: on_device(): jnp.einsum('pkj,pjx->pkx', same.astype(jnp.float32), contrib.reshape(peer...]
    reshape x2 -> x0, local copies, waits for them, and re-layouts: 14 us -> none  [the longest x1 7.05 us: on_device(): contrib.reshape(peers, capacity, samples * width)]
    scatter x1 -> x0, local copies, waits for them, and re-layouts: 8.07 us -> none  [on_device(): send_rows = jnp.zeros((peers * capacity, block_width, width), jnp.bfloat1...]
    dot_general x1 -> x0, local copies, waits for them, and re-layouts: 6.4 us -> none  [on_device(): jnp.einsum('kt,kx->tx', owner, rounded.reshape(peers * capacity, samples...]
  transfers between devices with their start and end apart: 4 -> 0, of which waited for: 1 -> 0; matrix products, arithmetic and copies ran while one was open for 33% -> 0% of each run, Pallas kernels for 0% -> 0%
where the time goes in v2:
time: 102 us; the launch traced here: 100 us
  Pallas kernels  96.8 us (95%)
  local copies, waits for them, and re-layouts  2.14 us (2%)
  between operations  1.4 us (1%)
    pallas_call x1, Pallas kernels, exchange(): pl.pallas_call(functools.partial(exchange_kernel, tight, peers), out_shap...  83.5 us
    pallas_call x1, Pallas kernels, cross(): pl.pallas_call(cross_kernel, out_shape=jax.ShapeDtypeStruct((samples, wid...  9.43 us
    pallas_call x1, Pallas kernels, prep(): pl.pallas_call(functools.partial(prep_kernel, tight), out_shape=(jax.Shap...  3.8 us

profile of v2, /device:TPU:8, one launch (start us, length us, event | category | flops | bytes accessed | tf_op | source)
XLA Modules:
  0.0 100.3 jit_solution(11984464038802891898)
XLA Ops:
  0.7 3.8 %prep_tight.1 = (s32[8,128]{1,0:T(8,128)}, f32[128,128]{1,0:T(8,128)}, f32[128,128]{1,0:T(8,128)}, f32[128,128]{1,0:T(8,128)}, f32[128,128]{1,0:T(8,128)}, /*index=5*/bf16[256,128]{1,0:T(8,128)(2,1)}, f32[8,128]{1,0:T(8,128)}) custom-call(s32[1]{0:T(128)S(6)} %copy.21.count_ref, s32[64,128]{1,0:T(8,128)} %rows_ref.1, s32[64,128]{1,0:T(8,128)} %slots_ref.1, ...), custom_call_target="tpu_custom_call" | custom-call | tf_op jit(solution)/shard_map/prep_tight/pallas_call | solution.py:114
  4.5 0.0 copy-start
  4.5 0.0 copy-start.1
  4.5 0.0 copy-start.2
  4.5 0.0 copy-start.3
  4.5 0.0 copy-start.4
  4.5 83.5 %exchange_tight.1 = (bf16[32,512,128]{2,1,0:T(8,128)(2,1)}, f32[32,8,128]{2,1,0:T(8,128)S(1)}, f32[8,128]{1,0:T(8,128)}, bf16[4,2560,256]{2,1,0:T(8,128)(2,1)}, bf16[4,2560,256]{2,1,0:T(8,128)(2,1)}) custom-call(s32[8,128]{1,0:T(8,128)} %get-tuple-element.64.refs_0_, bf16[20,2048,128]{2,1,0:T(8,128)(2,1)} %refs_1_.1, f32[128,128]{1,0:T(8,128)} %get-tuple-element.65.refs_2_, ...), custom_call_target="tpu_custom_call" | custom-call | tf_op jit(solution)/shard_map/exchange_tight/pallas_call | solution.py:439
  88.0 1.2 %slice.12 = f32[1,1]{1,0:T(1,128)} slice(f32[8,128]{1,0:T(8,128)} %get-tuple-element.71), slice={[0:1], [0:1]} | slice | bytes 8 | tf_op jit(solution)/shard_map/slice | solution.py:549
  89.9 0.0 copy-done
  89.9 0.0 copy-done.1
  89.9 0.0 copy-done.2
  89.9 0.0 copy-done.3
  89.9 0.0 copy-done.4
  89.9 0.2 copy.15
  90.2 0.7 copy.16.tab_ref
  90.9 9.4 %cross.1 = bf16[128,2560]{1,0:T(8,128)(2,1)} custom-call(s32[32,4]{1,0:T(8,128)} %copy.16.tab_ref, bf16[32,512,128]{2,1,0:T(8,128)(2,1)} %get-tuple-element.75.got_ref, bf16[4,256,256]{2,1,0:T(8,128)(2,1)} %mix_ref.1, f32[4,2560]{1,0:T(4,128)} %bias_ref.1, bf16[4,2560]{1,0:T(4,128)(2,1)} %gate_ref.1, bf16[4,2560,256]{2,1,0:T(8,128)(2,1)} %get-tuple-element.76.win_hbm, ...), custom_call_target="tpu_custom_call" | custom-call | tf_op jit(solution)/shard_map/cross/pallas_call | solution.py:501
  (2 shorter events, 0.0 us)
Async XLA Ops:
  4.5 85.4 %copy-start = (s32[64,128]{1,0:T(8,128)S(1)}, s32[64,128]{1,0:T(8,128)}, u32[]{:S(2)}) copy-start(s32[64,128]{1,0:T(8,128)} %rows_ref.1) | copy-start | bytes 98308
  4.5 85.4 %copy-start.1 = (s32[64,128]{1,0:T(8,128)S(1)}, s32[64,128]{1,0:T(8,128)}, u32[]{:S(2)}) copy-start(s32[64,128]{1,0:T(8,128)} %slots_ref.1) | copy-start | bytes 98308
  4.5 85.4 %copy-start.2 = (s32[64]{0:T(128)S(1)}, s32[64]{0:T(128)}, u32[]{:S(2)}) copy-start(s32[64]{0:T(128)} %param.17) | copy-start | bytes 772
  4.5 85.4 %copy-start.3 = (s32[64,1]{0,1:T(1,128)S(1)}, s32[64,1]{0,1:T(1,128)}, u32[]{:S(2)}) copy-start(s32[64,1]{0,1:T(1,128)} %param.18) | copy-start | bytes 772
  4.5 85.4 %copy-start.4 = (s32[64]{0:T(128)S(1)}, s32[64]{0:T(128)}, u32[]{:S(2)}) copy-start(s32[64]{0:T(128)} %param.19) | copy-start | bytes 772
